TPU v7x, 32 devices: a whole 2x2x4 slice. The times are simulated.
32 devices in a mesh: parts: 2 (over y), replica: 4 (over x, core), tensor: 4 (over z).
Axes of the slice: x: 2, y: 2, z: 4, core: 2. Of those that a mesh axis runs over, the one named last changes fastest.
Arguments:
- prompt_owner: int32 [8], P('parts'), parts along dimension 0, may hold values from 0 to 3, each once
- fork_map: int32 [1024], P(('parts', 'replica')), parts along dimension 0, may hold values from 0 to 3
- page_table: int32 [24], P('parts'), parts along dimension 0, may hold values from 0 to 11, each once
- prompt_length: int32 [8], P('parts'), parts along dimension 0, may hold values from 1 to 384
- span_states: bfloat16 [1024, 8192], P(('parts', 'replica'), 'tensor'), parts along dimension 0, may hold values from -6 to 6
- decode_states: bfloat16 [1024, 4, 8192], P(('parts', 'replica'), None, 'tensor'), parts along dimension 0, may hold values from -6 to 6
- decode_queries: bfloat16 [1024, 4, 4096], P(('parts', 'replica'), None, 'tensor'), parts along dimension 0, may hold values from -64 to 64
- key_weight: bfloat16 [8192, 512], P('tensor'), may hold values from -0.0625 to 0.0625
- value_weight: bfloat16 [8192, 512], P('tensor'), may hold values from -0.0625 to 0.0625
- out_weight: bfloat16 [4096, 8192], P(None, 'tensor'), may hold values from -0.09375 to 0.09375
- page_pool: bfloat16 [4, 24, 128, 256], P('tensor', 'parts'), parts along dimension 1, may hold values from -6 to 60, as said below
Outputs:
- decoded: bfloat16 [1024, 4, 8192], P(('parts', 'replica'), None, 'tensor'), parts along dimension 0
There are 2 independent parts, one for each index of `parts`. A program takes and returns all parts, laid end to end along the dimension named above; an argument that names none is the same for every part. Nothing has to cross between parts.
Inputs may be any that keep to these rules, and one draw needn't show every extreme that they name: Replica r prefills prompt prompt_owner[r]; every prompt has exactly one such replica. The cache pages of prompt p are page_table[p * 3 + c] for c below 3; every pool page belongs to exactly one prompt. page_pool[t] holds the cache of key-value head t; devices that read the same head hold equal copies.
All inputs are finite; a program needn't handle non-finite values.
Results may differ from a plain program's by a relative error of at most 0.009.
Values may be sent and summed in bfloat16 or wider, within the bound.
A program may use at most 64 MiB of HBM per device.

v0:
```python
import math

import jax
import jax.numpy as jnp
from jax import lax
from jax.sharding import PartitionSpec as P

HD = 128


rope_base = 1000000.0


def rotary(vectors, places):
    half = vectors.shape[-1] // 2
    freq = rope_base ** (-(2.0 / vectors.shape[-1]) * jnp.arange(half, dtype=jnp.float32))
    angle = places.astype(jnp.float32)[..., None, None] * freq
    cosine = jnp.cos(angle)
    sine = jnp.sin(angle)
    first = vectors[..., :half]
    second = vectors[..., half:]
    return jnp.concatenate([first * cosine - second * sine, second * cosine + first * sine], -1)


def rotate_round(summed, places, kv_heads):
    number = summed.shape[0]
    turned = rotary(summed[:, : kv_heads * HD].reshape(number, kv_heads, HD), places)
    turned = turned.astype(jnp.bfloat16).reshape(number, kv_heads * HD)
    return jnp.concatenate([turned, summed[:, kv_heads * HD :].astype(jnp.bfloat16)], 1)


def own_pair(packed, head_group, kv_heads):
    key_part = lax.dynamic_slice_in_dim(packed, head_group * HD, HD, 1)
    value_part = lax.dynamic_slice_in_dim(packed, (kv_heads + head_group) * HD, HD, 1)
    return jnp.concatenate([key_part, value_part], 1)


def on_device(
    prompt_owner,
    fork_map,
    page_table,
    prompt_length,
    span_states,
    decode_states,
    decode_queries,
    key_weight,
    value_weight,
    out_weight,
    page_pool,
):
    replica = lax.axis_index("replica")
    device_rank = lax.axis_index("tensor")
    n_replica = lax.axis_size("replica")
    n_tensor = lax.axis_size("tensor")
    span = span_states.shape[0]
    rows, steps, width = decode_states.shape
    heads_dev = decode_queries.shape[2] // HD
    kv_heads = key_weight.shape[1] // HD
    sharing = n_tensor // kv_heads
    prompts = jnp.arange(n_replica, dtype=jnp.int32)
    own_prompt = jnp.sum(jnp.where(prompts == replica, prompt_owner, 0))
    own_length = jnp.sum(jnp.where(prompts == own_prompt, prompt_length, 0))
    row_hits = fork_map[:, None] == prompts[None, :]
    row_length = jnp.sum(jnp.where(row_hits, prompt_length[None, :], 0), 1)
    positions = jnp.concatenate(
        [
            own_length + jnp.arange(span, dtype=jnp.int32),
            (row_length[:, None] + span + jnp.arange(steps, dtype=jnp.int32)[None, :]).reshape(-1),
        ]
    )
    tokens = jnp.concatenate([span_states, decode_states.reshape(rows * steps, width)], 0)
    projected = jnp.dot(
        tokens, jnp.concatenate([key_weight, value_weight], 1), preferred_element_type=jnp.float32
    )
    share = lax.psum_scatter(projected, "tensor", scatter_dimension=0, tiled=True)
    number = share.shape[0]
    start = device_rank * number
    places = lax.dynamic_slice_in_dim(positions, start, number)
    turned = rotate_round(share, places, kv_heads)
    groups = jnp.stack(
        [own_pair(turned, group_index, kv_heads) for group_index in range(kv_heads)], 0
    )
    outgoing = jnp.repeat(groups, sharing, axis=0)
    paired = lax.all_to_all(outgoing, "tensor", split_axis=0, concat_axis=1, tiled=True).reshape(
        -1, 2 * HD
    )
    arrived = lax.all_gather(paired[:span], "replica", axis=0, tiled=True)
    tail_pair = paired[span:].reshape(rows, steps, 2 * HD)
    pool_pages = page_table.shape[0]
    cpages = pool_pages // n_replica
    page_size = page_pool.shape[2]
    entries = jnp.arange(pool_pages, dtype=jnp.int32)
    page_hits = page_table[None, :] == entries[:, None]
    page_prompt = jnp.sum(jnp.where(page_hits, entries[None, :] // cpages, 0), 1)
    page_slot = jnp.sum(jnp.where(page_hits, entries[None, :] % cpages, 0), 1)
    page_length = jnp.sum(
        jnp.where(page_prompt[:, None] == prompts[None, :], prompt_length[None, :], 0), 1
    )
    visible = (
        page_slot[:, None] * page_size + jnp.arange(page_size, dtype=jnp.int32)[None, :]
        < page_length[:, None]
    )
    pool_prompt = jnp.where(visible, page_prompt[:, None], -1).reshape(-1)
    key_prompt = jnp.concatenate([pool_prompt, jnp.repeat(prompt_owner, span)])
    key_table = jnp.concatenate([page_pool.reshape(-1, 2 * HD), arrived], 0)
    cached_keys = key_table[:, :HD]
    cached_values = key_table[:, HD:]
    scale = 1.0 / math.sqrt(HD)
    causal = jnp.arange(steps)[None, :] <= jnp.arange(steps)[:, None]
    per_block = max(1, min(rows, 512 // (steps * heads_dev)))
    blocks = rows // per_block
    queries = decode_queries.reshape(blocks, per_block, steps, heads_dev, HD)

    def attend(items):
        query, prompt, own_tail = items
        flat = query.reshape(-1, HD)
        scores = (
            lax.dot_general(
                flat, cached_keys, (((1,), (1,)), ((), ())), preferred_element_type=jnp.float32
            )
            * scale
        )
        scores = scores.reshape(per_block, steps, heads_dev, -1)
        allowed = (key_prompt[None, :] == prompt[:, None])[:, None, None, :]
        scores = jnp.where(allowed, scores, -jnp.inf)
        tail_scores = (
            jnp.einsum(
                "rshd,rtd->rsht", query, own_tail[..., :HD], preferred_element_type=jnp.float32
            )
            * scale
        )
        tail_scores = jnp.where(causal[None, :, None, :], tail_scores, -jnp.inf)
        highest = jnp.maximum(jnp.max(scores, -1), jnp.max(tail_scores, -1))
        weight = jnp.exp(scores - highest[..., None])
        tail_weight = jnp.exp(tail_scores - highest[..., None])
        total = jnp.sum(weight, -1) + jnp.sum(tail_weight, -1)
        rounded = weight.astype(jnp.bfloat16).reshape(-1, weight.shape[-1])
        mixed = jnp.dot(rounded, cached_values, preferred_element_type=jnp.float32).reshape(
            per_block, steps, heads_dev, HD
        )
        mixed = mixed + jnp.einsum(
            "rsht,rtd->rshd",
            tail_weight.astype(jnp.bfloat16),
            own_tail[..., HD:],
            preferred_element_type=jnp.float32,
        )
        return (mixed / total[..., None]).astype(jnp.bfloat16)

    attended = lax.map(
        attend,
        (
            queries,
            fork_map.reshape(blocks, per_block),
            tail_pair.reshape(blocks, per_block, steps, 2 * HD),
        ),
    )
    head_rows = attended.reshape(rows * steps, heads_dev * HD)
    decoded = jnp.dot(
        lax.all_gather(head_rows, "tensor", axis=1, tiled=True),
        out_weight,
        preferred_element_type=jnp.float32,
    )
    return decoded.astype(jnp.bfloat16).reshape(rows, steps, width)


def solution(mesh):
    in_specs = (
        P("parts"),
        P(("parts", "replica")),
        P("parts"),
        P("parts"),
        P(("parts", "replica"), "tensor"),
        P(("parts", "replica"), None, "tensor"),
        P(("parts", "replica"), None, "tensor"),
        P("tensor", None),
        P("tensor", None),
        P(None, "tensor"),
        P("tensor", "parts", None, None),
    )
    out_specs = P(("parts", "replica"), None, "tensor")
    return jax.shard_map(
        on_device, mesh=mesh, in_specs=in_specs, out_specs=out_specs, check_vma=False
    )
```

profile of v0, /device:TPU:0, one launch (start us, length us, event | category | flops | bytes accessed | tf_op | source)
XLA Modules:
  0.0 287.4 jit_solution(17517306770796353733)
XLA Ops:
  6.5 2.6 reshape.220
  9.2 6.6 %fusion.18 = f32[640,1024]{1,0:T(8,128)} fusion(bf16[2048,512]{1,0:T(8,128)(2,1)} %param.21, bf16[2048,512]{1,0:T(8,128)(2,1)} %param.20, bf16[512,2048]{1,0:T(8,128)(2,1)S(1)} %reshape.220, bf16[128,2048]{1,0:T(8,128)(2,1)S(1)} %copy-done.5), kind=kOutput, calls=%fused_computation.28 | convolution fusion | flops 2697986048 | bytes 9437184 | tf_op jit(solution)/shard_map/dot_general | solution.py:72
  19.3 51.6 %reduce-scatter.2.cloned.1.call-done = f32[160,1024]{1,0:T(8,128)} async-done(((f32[640,1024]{1,0:T(8,128)}), f32[160,1024]{1,0:T(8,128)}) %reduce-scatter.2.cloned.1.call-update) | async-done | bytes 655376 | tf_op jit(solution)/shard_map/reduce_scatter | solution.py:75
  74.8 3.5 %all-to-all-start = ((bf16[4,160,256]{2,1,0:T(8,128)(2,1)}), bf16[4,160,256]{2,1,0:T(8,128)(2,1)S(1)}, u32[]{:S(2)}, u32[]{:S(2)}) async-start(bf16[4,160,256]{2,1,0:T(8,128)(2,1)} %pad_maximum_fusion.1), calls=%async_computation.1 | async-start | bytes 655360 | tf_op jit(solution)/shard_map/all_to_all | solution.py:84
  79.8 8.6 %all-to-all-done = bf16[4,160,256]{2,1,0:T(8,128)(2,1)S(1)} async-done(((bf16[4,160,256]{2,1,0:T(8,128)(2,1)}), bf16[4,160,256]{2,1,0:T(8,128)(2,1)S(1)}, u32[]{:S(2)}, u32[]{:S(2)}) %all-to-all-start) | async-done | bytes 327712 | tf_op jit(solution)/shard_map/all_to_all | solution.py:84
  88.4 5.8 %all_gather.6 = bf16[512,256]{1,0:T(8,128)(2,1)S(1)} all-gather(bf16[128,256]{1,0:T(8,128)(2,1)S(1)} %slice.47), channel_id=1, replica_groups=mesh['parts'=2,'replica'=4,'tensor'=4] {'replica'}, dimensions={0}, use_global_device_ids=true | all-gather | bytes 327680 | tf_op jit(solution)/shard_map/all_gather | solution.py:87
  95.1 87.2 %while.11 = (s32[]{:T(128)}, bf16[8,16,4,8,128]{4,3,2,1,0:T(8,128)(2,1)}, s32[2048]{0:T(1024)S(1)}, s32[8,16]{1,0:T(8,128)S(1)}, bf16[8,16,4,8,128]{4,3,2,1,0:T(...) while((s32[]{:T(128)}, ...), condition=%wide.region_12.13_spmd.clone, body=%wide.region_7.12_spmd.clone.sunk | while | flops 546551296 | bytes 15242553 | solution.py:149
  96.2 2.7 fusion.56
  99.7 3.3 %fusion.58 = (f32[512]{0:T(512)S(1)}, bf16[512,2048]{1,0:T(8,128)(2,1)S(1)}) fusion(f32[512,2048]{1,0:T(8,128)} %get-tuple-element.173, f32[512]{0:T(512)S(1)} %max.15, pred[16,2048]{1,0:T(8,128)(4,1)S(1)} %broadcast_compare_fusion.2), kind=kLoop, calls=%fused_computation.4.clone.1 | loop fusion | flops 5242368 | bytes 6328320 | tf_op jit(solution)/shard_map/while/body/eval_jaxpr/reduce_sum | solution.py:136
  103.6 2.4 fusion.60
  107.1 2.7 fusion.56
  110.6 3.3 %fusion.58 = (f32[512]{0:T(512)S(1)}, bf16[512,2048]{1,0:T(8,128)(2,1)S(1)}) fusion(f32[512,2048]{1,0:T(8,128)} %get-tuple-element.173, f32[512]{0:T(512)S(1)} %max.15, pred[16,2048]{1,0:T(8,128)(4,1)S(1)} %broadcast_compare_fusion.2), kind=kLoop, calls=%fused_computation.4.clone.1 | loop fusion | flops 5242368 | bytes 6328320 | tf_op jit(solution)/shard_map/while/body/eval_jaxpr/reduce_sum | solution.py:136
  118.0 2.7 fusion.56
  121.5 3.3 %fusion.58 = (f32[512]{0:T(512)S(1)}, bf16[512,2048]{1,0:T(8,128)(2,1)S(1)}) fusion(f32[512,2048]{1,0:T(8,128)} %get-tuple-element.173, f32[512]{0:T(512)S(1)} %max.15, pred[16,2048]{1,0:T(8,128)(4,1)S(1)} %broadcast_compare_fusion.2), kind=kLoop, calls=%fused_computation.4.clone.1 | loop fusion | flops 5242368 | bytes 6328320 | tf_op jit(solution)/shard_map/while/body/eval_jaxpr/reduce_sum | solution.py:136
  125.4 2.4 fusion.60
  128.9 2.7 fusion.56
  132.4 3.3 %fusion.58 = (f32[512]{0:T(512)S(1)}, bf16[512,2048]{1,0:T(8,128)(2,1)S(1)}) fusion(f32[512,2048]{1,0:T(8,128)} %get-tuple-element.173, f32[512]{0:T(512)S(1)} %max.15, pred[16,2048]{1,0:T(8,128)(4,1)S(1)} %broadcast_compare_fusion.2), kind=kLoop, calls=%fused_computation.4.clone.1 | loop fusion | flops 5242368 | bytes 6328320 | tf_op jit(solution)/shard_map/while/body/eval_jaxpr/reduce_sum | solution.py:136
  136.3 2.4 fusion.60
  139.8 2.7 fusion.56
  143.3 3.3 %fusion.58 = (f32[512]{0:T(512)S(1)}, bf16[512,2048]{1,0:T(8,128)(2,1)S(1)}) fusion(f32[512,2048]{1,0:T(8,128)} %get-tuple-element.173, f32[512]{0:T(512)S(1)} %max.15, pred[16,2048]{1,0:T(8,128)(4,1)S(1)} %broadcast_compare_fusion.2), kind=kLoop, calls=%fused_computation.4.clone.1 | loop fusion | flops 5242368 | bytes 6328320 | tf_op jit(solution)/shard_map/while/body/eval_jaxpr/reduce_sum | solution.py:136
  147.2 2.4 fusion.60
  150.7 2.7 fusion.56
  154.2 3.3 %fusion.58 = (f32[512]{0:T(512)S(1)}, bf16[512,2048]{1,0:T(8,128)(2,1)S(1)}) fusion(f32[512,2048]{1,0:T(8,128)} %get-tuple-element.173, f32[512]{0:T(512)S(1)} %max.15, pred[16,2048]{1,0:T(8,128)(4,1)S(1)} %broadcast_compare_fusion.2), kind=kLoop, calls=%fused_computation.4.clone.1 | loop fusion | flops 5242368 | bytes 6328320 | tf_op jit(solution)/shard_map/while/body/eval_jaxpr/reduce_sum | solution.py:136
  158.2 2.4 fusion.60
  161.6 2.7 fusion.56
  165.1 3.3 %fusion.58 = (f32[512]{0:T(512)S(1)}, bf16[512,2048]{1,0:T(8,128)(2,1)S(1)}) fusion(f32[512,2048]{1,0:T(8,128)} %get-tuple-element.173, f32[512]{0:T(512)S(1)} %max.15, pred[16,2048]{1,0:T(8,128)(4,1)S(1)} %broadcast_compare_fusion.2), kind=kLoop, calls=%fused_computation.4.clone.1 | loop fusion | flops 5242368 | bytes 6328320 | tf_op jit(solution)/shard_map/while/body/eval_jaxpr/reduce_sum | solution.py:136
  169.1 2.4 fusion.60
  172.5 2.7 fusion.56
  176.0 3.3 %fusion.58 = (f32[512]{0:T(512)S(1)}, bf16[512,2048]{1,0:T(8,128)(2,1)S(1)}) fusion(f32[512,2048]{1,0:T(8,128)} %get-tuple-element.173, f32[512]{0:T(512)S(1)} %max.15, pred[16,2048]{1,0:T(8,128)(4,1)S(1)} %broadcast_compare_fusion.2), kind=kLoop, calls=%fused_computation.4.clone.1 | loop fusion | flops 5242368 | bytes 6328320 | tf_op jit(solution)/shard_map/while/body/eval_jaxpr/reduce_sum | solution.py:136
  182.4 2.5 copy.19
  184.9 79.9 %all-gather.2.cloned.1.call-done = bf16[512,4096]{1,0:T(8,128)(2,1)} async-done(((bf16[512,1024]{1,0:T(8,128)(2,1)}), bf16[512,4096]{1,0:T(8,128)(2,1)}) %all-gather.2.cloned.1.call-update) | async-done | bytes 4194320 | tf_op jit(solution)/shard_map/all_gather | solution.py:159
  264.8 13.6 %convolution_convert_fusion = bf16[512,2048]{1,0:T(8,128)(2,1)S(1)} fusion(bf16[512,4096]{1,0:T(8,128)(2,1)} %all-gather.2.cloned.1.call-done, bf16[4096,2048]{1,0:T(8,128)(2,1)} %param.22), kind=kOutput, calls=%fused_computation.32 | convolution fusion | flops 8590983168 | bytes 23068672 | tf_op jit(solution)/shard_map/dot_general | solution.py:158
  (169 shorter events, 36.3 us)
Async XLA Ops:
  6.5 2.6 copy-start.5
  6.5 64.5 %reduce-scatter.2.cloned.1.call-start = ((), (), s32[]{:S(2)}) async-start(), calls=%async_computation.2 | async-start | bytes 3276800 | tf_op jit(solution)/shard_map/reduce_scatter | solution.py:75
  9.1 6.7 %copy-start.4 = (s32[128]{0:T(128)S(1)}, s32[128]{0:T(128)}, u32[]{:S(2)}) copy-start(s32[128]{0:T(128)} %param.14) | copy-start | bytes 1540
  9.2 6.7 %copy-start.6 = (s32[4]{0:T(128)S(1)}, s32[4]{0:T(128)}, u32[]{:S(2)}) copy-start(s32[4]{0:T(128)} %param.16) | copy-start | bytes 52
  9.2 7.0 %copy-start.3 = (s32[4]{0:T(128)S(1)}, s32[4]{0:T(128)}, u32[]{:S(2)}) copy-start(s32[4]{0:T(128)} %param.13) | copy-start | bytes 52
  9.2 9.6 %copy-start.2 = (s32[12]{0:T(128)S(1)}, s32[12]{0:T(128)}, u32[]{:S(2)}) copy-start(s32[12]{0:T(128)} %param.15) | copy-start | bytes 148
  15.8 62.5 %copy-start = (bf16[128,4,1024]{2,1,0:T(4,128)(2,1)S(1)}, bf16[128,4,1024]{2,1,0:T(4,128)(2,1)}, u32[]{:S(2)}) copy-start(bf16[128,4,1024]{2,1,0:T(4,128)(2,1)} %param.19) | copy-start | bytes 3145732
  72.5 21.8 %copy-start.1 = (bf16[1,12,128,256]{3,2,1,0:T(8,128)(2,1)S(1)}, bf16[1,12,128,256]{3,2,1,0:T(8,128)(2,1)}, u32[]{:S(2)}) copy-start(bf16[1,12,128,256]{3,2,1,0:T(8,128)(2,1)} %param.23) | copy-start | bytes 2359300
  74.8 13.6 %all-to-all-start = ((bf16[4,160,256]{2,1,0:T(8,128)(2,1)}), bf16[4,160,256]{2,1,0:T(8,128)(2,1)S(1)}, u32[]{:S(2)}, u32[]{:S(2)}) async-start(bf16[4,160,256]{2,1,0:T(8,128)(2,1)} %pad_maximum_fusion.1), calls=%async_computation.1 | async-start | bytes 655360 | tf_op jit(solution)/shard_map/all_to_all | solution.py:84
  78.2 186.6 %all-gather.2.cloned.1.call-start = ((), (), s32[]{:S(2)}) async-start(), calls=%async_computation.3 | async-start | bytes 5242880 | tf_op jit(solution)/shard_map/all_gather | solution.py:159
Sparse Core Ops, SparseCore 0:
  16.0 54.9 reduce-scatter.1
  185.0 79.7 all-gather.1
where the time goes:
time: 289 us; the launch traced here: 287 us
  waiting for transfers between devices  140 us (48%)
  matrix products  68.5 us (24%)
  other arithmetic  35.3 us (12%)
  local copies, waits for them, and re-layouts  20 us (7%)
  between operations  13.7 us (5%)
  blocking collectives  5.78 us (2%)
  starting transfers between devices  3.5 us (1%)
    all_gather x1, waiting for transfers between devices, on_device(): lax.all_gather(head_rows, 'tensor', axis=1, tiled=True)  79.9 us
    reduce_scatter x1, waiting for transfers between devices, on_device(): lax.psum_scatter(projected, 'tensor', scatter_dimension=0, tiled=True)  51.6 us
    reduce_sum x16, other arithmetic, attend(): total = jnp.sum(weight, -1) + jnp.sum(tail_weight, -1)  27.5 us
    dot_general x8, matrix products, attend(): lax.dot_general(flat, cached_keys, (((1,), (1,)), ((), ())), preferred_el...  21.3 us
    dot_general x8, matrix products, attend(): jnp.dot(rounded, cached_values, preferred_element_type=jnp.float32)  19.4 us
    dot_general x1, matrix products, on_device(): jnp.dot(lax.all_gather(head_rows, 'tensor', axis=1, tiled=True), out_weig...  13.6 us
    all_to_all x1, waiting for transfers between devices, on_device(): lax.all_to_all(outgoing, 'tensor', split_axis=0, concat_axis=1, tiled=True)  8.61 us
    dynamic_slice x8, local copies, waits for them, and re-layouts, on_device(): lax.map(attend, (queries, fork_map.reshape(blocks, per_block), tail_pair....  7.36 us
  transfers between devices with their start and end apart: 3, of which 3 were waited for; matrix products, arithmetic and copies ran while one was open for 2% of the time, Pallas kernels for 0%

commit v1 on v0

--- a/solution.py
+++ b/solution.py
@@ -1,8 +1,11 @@
+import functools
 import math
 
 import jax
 import jax.numpy as jnp
 from jax import lax
+from jax.experimental import pallas as pl
+from jax.experimental.pallas import tpu as pltpu
 from jax.sharding import PartitionSpec as P
 
 HD = 128
@@ -35,7 +38,7 @@
     return jnp.concatenate([key_part, value_part], 1)
 
 
-def on_device(
+def general(
     prompt_owner,
     fork_map,
     page_table,
@@ -163,6 +166,353 @@
     return decoded.astype(jnp.bfloat16).reshape(rows, steps, width)
 
 
+MESH_ID = pl.DeviceIdType.MESH
+TILE = 128
+FAR = -(2.0**100)
+
+
+def nt(left, right):
+    return lax.dot_general(
+        left, right, (((1,), (1,)), ((), ())), preferred_element_type=jnp.float32
+    )
+
+
+def fused(
+    n, n_rep, steps, tok, wk, wv, cosine, sine, query, hot, pool, far, w_hbm, out,
+    w_all, part, landed, own, span_all, keys, values, tail_key, tail_value, gathered, acc,
+    w_sem, rs_send, rs_recv, sp_send, sp_recv, ag_send, ag_recv,
+):
+    z = lax.axis_index("tensor")
+    rep = lax.axis_index("replica")
+    span = span_all.shape[1]
+    rows = query.shape[0]
+    width = query.shape[1]
+    heads = width // HD
+    cached = pool.shape[0]
+    blocks = tok.shape[0] // TILE
+    span_blocks = span // TILE
+    chunks = rows // TILE
+
+    w_copy = pltpu.make_async_copy(w_hbm, w_all, w_sem)
+    w_copy.start()
+    barrier = pltpu.get_barrier_semaphore()
+    for k in range(1, n):
+        pl.semaphore_signal(
+            barrier, inc=1, device_id={"tensor": lax.rem(z + k, n)}, device_id_type=MESH_ID
+        )
+    for k in range(1, n_rep):
+        pl.semaphore_signal(
+            barrier, inc=1, device_id={"replica": lax.rem(rep + k, n_rep)}, device_id_type=MESH_ID
+        )
+    pl.semaphore_wait(barrier, n + n_rep - 2)
+
+    def at(block):
+        return pl.ds(pl.multiple_of(block * TILE, TILE), TILE)
+
+    def rs_copy(k, block):
+        return pltpu.make_async_remote_copy(
+            src_ref=part.at[k - 1, at(block)],
+            dst_ref=landed.at[k - 1, at(block)],
+            send_sem=rs_send.at[k - 1, block],
+            recv_sem=rs_recv.at[k - 1, block],
+            device_id={"tensor": lax.rem(z + k, n)},
+            device_id_type=MESH_ID,
+        )
+
+    def project(block, owner):
+        column = pl.ds(pl.multiple_of(owner * HD, HD), HD)
+        weight = jnp.concatenate([wk[:, column], wv[:, column]], 1)
+        return jnp.dot(tok[at(block), :], weight, preferred_element_type=jnp.float32)
+
+    @pl.loop(0, blocks)
+    def _(block):
+        for k in range(1, n):
+            part[k - 1, at(block), :] = project(block, lax.rem(z + k, n)).astype(jnp.bfloat16)
+            rs_copy(k, block).start()
+
+    @pl.loop(0, blocks)
+    def _(block):
+        own[at(block), :] = project(block, z)
+
+    keys[:cached, :HD] = pool[:, :HD]
+    values[:cached, :HD] = pool[:, HD:]
+    keys[:, HD:] = far[...]
+    values[:, HD:] = jnp.ones((values.shape[0], HD), jnp.bfloat16)
+    tail_value[:, HD:] = jnp.ones((TILE, HD), jnp.bfloat16)
+
+    def reduced(block):
+        total = own[at(block), :]
+        for k in range(1, n):
+            rs_copy(k, block).wait_recv()
+            total = total + landed[k - 1, at(block), :].astype(jnp.float32)
+        key = total[:, :HD]
+        key = key * cosine[at(block), :] + pltpu.roll(key, HD // 2, 1) * sine[at(block), :]
+        return key.astype(jnp.bfloat16), total[:, HD:].astype(jnp.bfloat16)
+
+    @pl.loop(0, span_blocks)
+    def _(block):
+        key, value = reduced(block)
+        span_all[rep, at(block), :HD] = key
+        span_all[rep, at(block), HD:] = value
+
+    def sp_copy(k, whose):
+        return pltpu.make_async_remote_copy(
+            src_ref=span_all.at[whose],
+            dst_ref=span_all.at[whose],
+            send_sem=sp_send.at[k - 1],
+            recv_sem=sp_recv.at[k - 1],
+            device_id={"replica": lax.rem(rep + k, n_rep)},
+            device_id_type=MESH_ID,
+        )
+
+    for k in range(1, n_rep):
+        sp_copy(k, rep).start()
+    for k in range(1, n_rep):
+        sp_copy(k, lax.rem(rep - k + n_rep, n_rep)).wait_recv()
+    for p in range(n_rep):
+        keys[cached + p * span : cached + (p + 1) * span, :HD] = span_all[p, :, :HD]
+        values[cached + p * span : cached + (p + 1) * span, :HD] = span_all[p, :, HD:]
+
+    def ag_copy(side, distance, chunk, origin):
+        target = z + 1 if side == 0 else z - 1
+        return pltpu.make_async_remote_copy(
+            src_ref=gathered.at[origin, at(chunk)],
+            dst_ref=gathered.at[origin, at(chunk)],
+            send_sem=ag_send.at[side, distance - 1, chunk],
+            recv_sem=ag_recv.at[side, distance - 1, chunk],
+            device_id={"tensor": target},
+            device_id_type=MESH_ID,
+        )
+
+    line = lax.broadcasted_iota(jnp.int32, (TILE, TILE), 0)
+    lane = lax.broadcasted_iota(jnp.int32, (TILE, TILE), 1)
+    causal = (line // steps == lane // steps) & (lane <= line)
+    factor = math.log2(math.e) / math.sqrt(HD)
+
+    @pl.loop(0, chunks)
+    def _(chunk):
+        key, value = reduced(chunk + span_blocks)
+        tail_key[...] = key
+        tail_value[:, :HD] = value
+
+        @pl.loop(0, heads)
+        def _(head):
+            column = pl.ds(pl.multiple_of(head * HD, HD), HD)
+            asked = query[at(chunk), column]
+            scores = nt(jnp.concatenate([asked, hot[at(chunk), :]], 1), keys[...])
+            tail = jnp.where(causal, nt(asked, tail_key[...]), FAR)
+            highest = jnp.maximum(
+                jnp.max(scores, 1, keepdims=True), jnp.max(tail, 1, keepdims=True)
+            )
+            weight = jnp.exp2((scores - highest) * factor).astype(jnp.bfloat16)
+            tail_weight = jnp.exp2((tail - highest) * factor).astype(jnp.bfloat16)
+            mixed = jnp.dot(weight, values[...], preferred_element_type=jnp.float32) + jnp.dot(
+                tail_weight, tail_value[...], preferred_element_type=jnp.float32
+            )
+            gathered[z, at(chunk), column] = (mixed[:, :HD] / mixed[:, HD:]).astype(jnp.bfloat16)
+
+        @pl.when(z + 1 < n)
+        def _():
+            ag_copy(0, 1, chunk, z).start()
+
+        @pl.when(z > 0)
+        def _():
+            ag_copy(1, 1, chunk, z).start()
+
+    w_copy.wait()
+    tall = min(2 * TILE, rows)
+    per = tall // TILE
+    wide = min(512, out.shape[1])
+
+    def add(origin, half, first):
+        span_rows = pl.ds(pl.multiple_of(half * tall, tall), tall)
+        deep = pl.ds(pl.multiple_of(origin * width, width), width)
+
+        @pl.loop(0, out.shape[1] // wide)
+        def _(column):
+            cols = pl.ds(pl.multiple_of(column * wide, wide), wide)
+            term = jnp.dot(
+                gathered[origin, span_rows, :], w_all[deep, cols], preferred_element_type=jnp.float32
+            )
+            if first:
+                acc[span_rows, cols] = term
+            else:
+                acc[span_rows, cols] += term
+
+    @pl.loop(0, rows // tall)
+    def _(half):
+        add(z, half, True)
+
+    for distance in range(1, n):
+
+        @pl.loop(0, rows // tall)
+        def _(half):
+            for side, origin, inside, onward in (
+                (0, z - distance, z >= distance, z + 1 < n),
+                (1, z + distance, z + distance < n, z > 0),
+            ):
+                for piece in range(per):
+                    chunk = half * per + piece
+
+                    @pl.when(inside)
+                    def _():
+                        ag_copy(side, distance, chunk, origin).wait_recv()
+
+                    if distance < n - 1:
+
+                        @pl.when(inside & onward)
+                        def _():
+                            ag_copy(side, distance + 1, chunk, origin).start()
+
+            for side, origin, inside in (
+                (0, z - distance, z >= distance),
+                (1, z + distance, z + distance < n),
+            ):
+
+                @pl.when(inside)
+                def _():
+                    add(origin, half, False)
+
+    @pl.loop(0, chunks)
+    def _(chunk):
+        out[at(chunk), :] = acc[at(chunk), :].astype(jnp.bfloat16)
+
+    for k in range(1, n):
+
+        @pl.loop(0, blocks)
+        def _(block):
+            rs_copy(k, block).wait_send()
+
+    for k in range(1, n_rep):
+        sp_copy(k, rep).wait_send()
+    for distance in range(1, n):
+
+        @pl.loop(0, chunks)
+        def _(chunk):
+            @pl.when((z >= distance - 1) & (z + 1 < n))
+            def _():
+                ag_copy(0, distance, chunk, z - distance + 1).wait_send()
+
+            @pl.when((z + distance - 1 < n) & (z > 0))
+            def _():
+                ag_copy(1, distance, chunk, z + distance - 1).wait_send()
+
+
+def on_device(
+    prompt_owner,
+    fork_map,
+    page_table,
+    prompt_length,
+    span_states,
+    decode_states,
+    decode_queries,
+    key_weight,
+    value_weight,
+    out_weight,
+    page_pool,
+):
+    replica = lax.axis_index("replica")
+    n_replica = lax.axis_size("replica")
+    n_tensor = lax.axis_size("tensor")
+    span = span_states.shape[0]
+    rows, steps, width = decode_states.shape
+    heads_dev = decode_queries.shape[2] // HD
+    kv_heads = key_weight.shape[1] // HD
+    number = rows * steps
+    if (
+        kv_heads != n_tensor
+        or span % TILE
+        or number % TILE
+        or number % min(2 * TILE, number)
+        or TILE % steps
+        or n_replica > HD
+    ):
+        return general(
+            prompt_owner, fork_map, page_table, prompt_length, span_states, decode_states,
+            decode_queries, key_weight, value_weight, out_weight, page_pool,
+        )
+    prompts = jnp.arange(n_replica, dtype=jnp.int32)
+    own_prompt = jnp.sum(jnp.where(prompts == replica, prompt_owner, 0))
+    own_length = jnp.sum(jnp.where(prompts == own_prompt, prompt_length, 0))
+    row_hits = fork_map[:, None] == prompts[None, :]
+    row_length = jnp.sum(jnp.where(row_hits, prompt_length[None, :], 0), 1)
+    positions = jnp.concatenate(
+        [
+            own_length + jnp.arange(span, dtype=jnp.int32),
+            (row_length[:, None] + span + jnp.arange(steps, dtype=jnp.int32)[None, :]).reshape(-1),
+        ]
+    )
+    half = HD // 2
+    freq = rope_base ** (-(2.0 / HD) * jnp.arange(half, dtype=jnp.float32))
+    angle = positions.astype(jnp.float32)[:, None] * freq
+    cosine = jnp.cos(angle)
+    sine = jnp.sin(angle)
+    cosine = jnp.concatenate([cosine, cosine], 1)
+    sine = jnp.concatenate([-sine, sine], 1)
+    tokens = jnp.concatenate([span_states, decode_states.reshape(number, width)], 0)
+    pool_pages = page_table.shape[0]
+    cpages = pool_pages // n_replica
+    page_size = page_pool.shape[2]
+    entries = jnp.arange(pool_pages, dtype=jnp.int32)
+    page_hits = page_table[None, :] == entries[:, None]
+    page_prompt = jnp.sum(jnp.where(page_hits, entries[None, :] // cpages, 0), 1)
+    page_slot = jnp.sum(jnp.where(page_hits, entries[None, :] % cpages, 0), 1)
+    page_length = jnp.sum(
+        jnp.where(page_prompt[:, None] == prompts[None, :], prompt_length[None, :], 0), 1
+    )
+    visible = (
+        page_slot[:, None] * page_size + jnp.arange(page_size, dtype=jnp.int32)[None, :]
+        < page_length[:, None]
+    )
+    pool_prompt = jnp.where(visible, page_prompt[:, None], -1).reshape(-1)
+    key_prompt = jnp.concatenate([pool_prompt, jnp.repeat(prompt_owner, span)])
+    lanes = jnp.arange(HD, dtype=jnp.int32)
+    far = jnp.where(
+        (lanes[None, :] < n_replica) & (key_prompt[:, None] != lanes[None, :]), FAR, 0.0
+    ).astype(jnp.bfloat16)
+    hot = jnp.broadcast_to(
+        (fork_map[:, None] == lanes[None, :])[:, None, :], (rows, steps, HD)
+    ).reshape(number, HD).astype(jnp.bfloat16)
+    pool = page_pool.reshape(-1, 2 * HD)
+    query = decode_queries.reshape(number, heads_dev * HD)
+    features = out_weight.shape[1]
+    table = pool.shape[0] + n_replica * span
+    total = span + number
+    vmem = pl.BlockSpec(memory_space=pltpu.VMEM)
+    bf16, f32 = jnp.bfloat16, jnp.float32
+    decoded = pl.pallas_call(
+        functools.partial(fused, n_tensor, n_replica, steps),
+        name="fused",
+        out_shape=jax.ShapeDtypeStruct((number, features), bf16),
+        in_specs=[vmem] * 9 + [pl.BlockSpec(memory_space=pl.ANY)],
+        out_specs=vmem,
+        scratch_shapes=[
+            pltpu.VMEM(out_weight.shape, bf16),
+            pltpu.VMEM((n_tensor - 1, total, 2 * HD), bf16),
+            pltpu.VMEM((n_tensor - 1, total, 2 * HD), bf16),
+            pltpu.VMEM((total, 2 * HD), f32),
+            pltpu.VMEM((n_replica, span, 2 * HD), bf16),
+            pltpu.VMEM((table, 2 * HD), bf16),
+            pltpu.VMEM((table, 2 * HD), bf16),
+            pltpu.VMEM((TILE, HD), bf16),
+            pltpu.VMEM((TILE, 2 * HD), bf16),
+            pltpu.VMEM((n_tensor, number, heads_dev * HD), bf16),
+            pltpu.VMEM((number, features), f32),
+            pltpu.SemaphoreType.DMA,
+            pltpu.SemaphoreType.DMA((n_tensor - 1, total // TILE)),
+            pltpu.SemaphoreType.DMA((n_tensor - 1, total // TILE)),
+            pltpu.SemaphoreType.DMA((n_replica - 1,)),
+            pltpu.SemaphoreType.DMA((n_replica - 1,)),
+            pltpu.SemaphoreType.DMA((2, n_tensor - 1, number // TILE)),
+            pltpu.SemaphoreType.DMA((2, n_tensor - 1, number // TILE)),
+        ],
+        compiler_params=pltpu.CompilerParams(
+            collective_id=0, has_side_effects=True, vmem_limit_bytes=60 * 1024 * 1024
+        ),
+    )(tokens, key_weight, value_weight, cosine, sine, query, hot, pool, far, out_weight)
+    return decoded.reshape(rows, steps, features)
+
+
 def solution(mesh):
     in_specs = (
         P("parts"),

time: 289 us -> 142 us (0.49)
  waiting for transfers between devices: 140 us -> 0 us
  Pallas kernels: 0 us -> 120 us
  matrix products: 68.5 us -> 0 us
  other arithmetic: 35.3 us -> 12.5 us
  between operations: 13.7 us -> 0.08 us
  local copies, waits for them, and re-layouts: 20 us -> 9.24 us
  blocking collectives: 5.78 us -> 0 us
  starting transfers between devices: 3.5 us -> 0 us
    pallas_call x0 -> x1, Pallas kernels: none -> 120 us  [on_device(): pl.pallas_call(functools.partial(fused, n_tensor, n_replica, steps), name...]
    all_gather x1 -> x0, waiting for transfers between devices: 79.9 us -> none  [on_device(): lax.all_gather(head_rows, 'tensor', axis=1, tiled=True)]
    dot_general x34 -> x0, matrix products: 68.5 us -> none  [the longest x8 21.3 us: attend(): lax.dot_general(flat, cached_keys, (((1,), (1,)), ((), ())), preferred_el...]
    reduce_scatter x1 -> x0, waiting for transfers between devices: 51.6 us -> none  [on_device(): lax.psum_scatter(projected, 'tensor', scatter_dimension=0, tiled=True)]
    reduce_sum x16 -> x0, other arithmetic: 27.5 us -> none  [attend(): total = jnp.sum(weight, -1) + jnp.sum(tail_weight, -1)]
    all_to_all x1 -> x0, waiting for transfers between devices: 8.61 us -> none  [on_device(): lax.all_to_all(outgoing, 'tensor', split_axis=0, concat_axis=1, tiled=True)]
    dynamic_slice x10 -> x0, local copies, waits for them, and re-layouts: 7.42 us -> none  [the longest x8 7.36 us: on_device(): lax.map(attend, (queries, fork_map.reshape(blocks, per_block), tail_pair....]
    all_gather x1 -> x0, blocking collectives: 5.78 us -> none  [on_device(): arrived = lax.all_gather(paired[:span], 'replica', axis=0, tiled=True)]
  transfers between devices with their start and end apart: 3 -> 0, of which waited for: 3 -> 0; matrix products, arithmetic and copies ran while one was open for 2% -> 0% of each run, Pallas kernels for 0% -> 0%
where the time goes in v1:
time: 142 us
  Pallas kernels  120 us (85%)
  other arithmetic  12.5 us (9%)
  local copies, waits for them, and re-layouts  9.24 us (7%)
    pallas_call x1, Pallas kernels, on_device(): pl.pallas_call(functools.partial(fused, n_tensor, n_replica, steps), name...  120 us
    reshape x1, local copies, waits for them, and re-layouts, on_device(): return decoded.reshape(rows, steps, features)  4.1 us

profile of v1, /device:TPU:0, one launch (start us, length us, event | category | flops | bytes accessed | tf_op | source)
XLA Modules:
  0.0 141.5 jit_solution(18003874679341725483)
XLA Ops:
  0.0 0.0 copy-start
  0.0 1.4 fusion.3
  1.4 2.0 %fusion.4 = s32[]{:T(128)} fusion(s32[4]{0:T(128)} %param.14, s32[]{:T(128)} %fusion.3), kind=kLoop, calls=%fused_computation.31 | loop fusion | flops 11 | bytes 24 | tf_op jit(solution)/shard_map/reduce_sum | solution.py:436
  3.4 0.7 iota_add_fusion.1
  4.1 0.8 select_reduce_fusion.3
  4.9 0.8 select_reduce_fusion.1
  5.7 0.7 select_reduce_fusion.2
  6.4 0.7 broadcast_bitcast_fusion
  7.1 0.1 select_bitcast_fusion
  7.2 0.7 fusion.2
  8.0 0.1 iota_add_fusion
  8.1 0.1 add.74
  8.2 0.7 broadcast_in_dim.102
  8.9 1.2 select_convert_fusion.far
  10.0 1.2 fusion.1
  11.2 1.1 pad_maximum_fusion.1
  12.3 0.0 copy-done
  12.3 0.0 copy-start.1
  12.4 1.1 reshape.121.query
  13.4 2.5 %reshape.120 = bf16[512,2048]{1,0:T(8,128)(2,1)S(1)} reshape(bf16[128,4,2048]{2,1,0:T(4,128)(2,1)} %param.16) | data formatting | bytes 4194304 | tf_op jit(solution)/shard_map/reshape | solution.py:452
  16.0 0.0 copy-done.1
  16.0 1.7 %pad_maximum_fusion.tok = bf16[640,2048]{1,0:T(8,128)(2,1)} fusion(bf16[512,2048]{1,0:T(8,128)(2,1)S(1)} %reshape.120, bf16[128,2048]{1,0:T(8,128)(2,1)S(1)} %copy-done.1), kind=kLoop, calls=%fused_computation | loop fusion | flops 5242880 | bytes 5242880 | tf_op jit(solution)/shard_map/concatenate | solution.py:452
  17.7 119.8 %fused.1 = bf16[512,2048]{1,0:T(8,128)(2,1)} custom-call(bf16[640,2048]{1,0:T(8,128)(2,1)} %pad_maximum_fusion.tok, bf16[2048,512]{1,0:T(8,128)(2,1)} %wk.1, bf16[2048,512]{1,0:T(8,128)(2,1)} %wv.1, f32[640,128]{1,0:T(8,128)} %get-tuple-element.10.cosine, f32[640,128]{1,0:T(8,128)} %get-tuple-element.11.sine, bf16[512,1024]{1,0:T(8,128)(2,1)} %reshape.121.query, ...), custom_call_target="tpu_custom_call" | custom-call | tf_op jit(solution)/shard_map/fused/pallas_call | solution.py:483
  137.4 4.1 %reshape.124 = bf16[128,4,2048]{2,1,0:T(4,128)(2,1)} reshape(bf16[512,2048]{1,0:T(8,128)(2,1)} %fused.1) | data formatting | bytes 4194304 | tf_op jit(solution)/shard_map/reshape | solution.py:513
  (7 shorter events, 0.1 us)
Async XLA Ops:
  0.0 12.3 %copy-start = (bf16[128,4,1024]{2,1,0:T(4,128)(2,1)S(1)}, bf16[128,4,1024]{2,1,0:T(4,128)(2,1)}, u32[]{:S(2)}) copy-start(bf16[128,4,1024]{2,1,0:T(4,128)(2,1)} %param.17) | copy-start | bytes 3145732
  12.3 3.6 %copy-start.1 = (bf16[128,2048]{1,0:T(8,128)(2,1)S(1)}, bf16[128,2048]{1,0:T(8,128)(2,1)}, u32[]{:S(2)}) copy-start(bf16[128,2048]{1,0:T(8,128)(2,1)} %param.15) | copy-start | bytes 1572868

commit v2 on v1

--- a/solution.py
+++ b/solution.py
@@ -3,6 +3,7 @@
 
 import jax
 import jax.numpy as jnp
+import numpy as np
 from jax import lax
 from jax.experimental import pallas as pl
 from jax.experimental.pallas import tpu as pltpu
@@ -178,23 +179,35 @@
 
 
 def fused(
-    n, n_rep, steps, tok, wk, wv, cosine, sine, query, hot, pool, far, w_hbm, out,
-    w_all, part, landed, own, span_all, keys, values, tail_key, tail_value, gathered, acc,
-    w_sem, rs_send, rs_recv, sp_send, sp_recv, ag_send, ag_recv,
+    n, n_rep, steps, owner_of, forks, table, length, freq, first_tok, wk, wv,
+    decode_hbm, query_hbm, pool_hbm, w_hbm, out,
+    w_all, later_tok, query, pool, tok, cosine, sine, hot, mine, part, landed, span_all,
+    keys, values, tail_key, tail_value, asked_all, gathered, acc,
+    in_sem, rs_send, rs_recv, sp_send, sp_recv, ag_send, ag_recv,
 ):
     z = lax.axis_index("tensor")
     rep = lax.axis_index("replica")
     span = span_all.shape[1]
     rows = query.shape[0]
-    width = query.shape[1]
+    number = rows * steps
+    width = query.shape[2]
     heads = width // HD
-    cached = pool.shape[0]
-    blocks = tok.shape[0] // TILE
+    pages, page_size = pool.shape[0], pool.shape[1]
+    cpages = pages // n_rep
+    cached = pages * page_size
     span_blocks = span // TILE
-    chunks = rows // TILE
-
-    w_copy = pltpu.make_async_copy(w_hbm, w_all, w_sem)
-    w_copy.start()
+    chunks = number // TILE
+    blocks = span_blocks + chunks
+    sampled = TILE // steps
+
+    loads = [
+        pltpu.make_async_copy(source, target, in_sem.at[index])
+        for index, (source, target) in enumerate(
+            ((decode_hbm, later_tok), (query_hbm, query), (pool_hbm, pool), (w_hbm, w_all))
+        )
+    ]
+    for load in loads:
+        load.start()
     barrier = pltpu.get_barrier_semaphore()
     for k in range(1, n):
         pl.semaphore_signal(
@@ -209,42 +222,132 @@
     def at(block):
         return pl.ds(pl.multiple_of(block * TILE, TILE), TILE)
 
-    def rs_copy(k, block):
+    def rs_copy(side, owner, block):
         return pltpu.make_async_remote_copy(
-            src_ref=part.at[k - 1, at(block)],
-            dst_ref=landed.at[k - 1, at(block)],
-            send_sem=rs_send.at[k - 1, block],
-            recv_sem=rs_recv.at[k - 1, block],
-            device_id={"tensor": lax.rem(z + k, n)},
+            src_ref=part.at[owner, at(block)],
+            dst_ref=landed.at[side, owner, at(block)],
+            send_sem=rs_send.at[owner, block],
+            recv_sem=rs_recv.at[side, owner, block],
+            device_id={"tensor": z + 1 if side == 0 else z - 1},
             device_id_type=MESH_ID,
         )
 
-    def project(block, owner):
+    tok[:span, :] = first_tok[...]
+    loads[0].wait()
+
+    @pl.loop(0, chunks)
+    def _(chunk):
+        tok[at(chunk + span_blocks), :] = later_tok[pl.ds(chunk * sampled, sampled)].reshape(
+            TILE, tok.shape[1]
+        )
+
+    @pl.loop(0, n)
+    def _(index):
+        owner = lax.rem(z + n - 1 - index, n)
         column = pl.ds(pl.multiple_of(owner * HD, HD), HD)
         weight = jnp.concatenate([wk[:, column], wv[:, column]], 1)
-        return jnp.dot(tok[at(block), :], weight, preferred_element_type=jnp.float32)
-
-    @pl.loop(0, blocks)
-    def _(block):
-        for k in range(1, n):
-            part[k - 1, at(block), :] = project(block, lax.rem(z + k, n)).astype(jnp.bfloat16)
-            rs_copy(k, block).start()
-
-    @pl.loop(0, blocks)
-    def _(block):
-        own[at(block), :] = project(block, z)
-
-    keys[:cached, :HD] = pool[:, :HD]
-    values[:cached, :HD] = pool[:, HD:]
-    keys[:, HD:] = far[...]
+        mine[owner] = jnp.dot(tok[...], weight, preferred_element_type=jnp.float32)
+        for side, edge in ((0, z == 0), (1, z == n - 1)):
+
+            @pl.when(edge & (index < n - 1))
+            def _():
+                part[owner] = mine[owner].astype(jnp.bfloat16)
+                for block in range(blocks):
+                    rs_copy(side, owner, block).start()
+
+    def onward(side, block):
+        for k in range(n - 1, 0, -1):
+            owner = z + k if side == 0 else z - k
+            inner = (z > 0) & (owner < n) if side == 0 else (z < n - 1) & (owner >= 0)
+
+            @pl.when(inner)
+            def _():
+                rs_copy(side, owner, block).wait_recv()
+                total = mine[owner, at(block), :] + landed[side, owner, at(block), :].astype(
+                    jnp.float32
+                )
+                part[owner, at(block), :] = total.astype(jnp.bfloat16)
+                rs_copy(side, owner, block).start()
+
+    def forward(block):
+        @pl.when(z < n // 2)
+        def _():
+            onward(0, block)
+            onward(1, block)
+
+        @pl.when(z >= n // 2)
+        def _():
+            onward(1, block)
+            onward(0, block)
+
+    line = lax.broadcasted_iota(jnp.int32, (TILE, TILE), 0)
+    lane = lax.broadcasted_iota(jnp.int32, (TILE, TILE), 1)
+    turn = jnp.where(lane < HD // 2, -1.0, 1.0)
+
+    def angles(block, places):
+        angle = places.astype(jnp.float32) * freq[:1, :]
+        cosine[at(block), :] = jnp.cos(angle)
+        sine[at(block), :] = jnp.sin(angle) * turn
+
+    own_length = length[owner_of[rep]]
+    for block in range(span_blocks):
+        angles(block, own_length + block * TILE + line)
+
+    forward(0)
+
+    group = 8 // math.gcd(8, steps)
+    small = lax.broadcasted_iota(jnp.int32, (group * steps, HD), 0)
+
+    @pl.loop(0, rows // group)
+    def _(item):
+        prompt = jnp.full((group * steps, HD), forks[item * group], jnp.int32)
+        for offset in range(1, group):
+            prompt = jnp.where(small >= offset * steps, forks[item * group + offset], prompt)
+        hot[pl.ds(pl.multiple_of(item * group * steps, 8), group * steps), :] = prompt
+
+    @pl.loop(0, chunks)
+    def _(chunk):
+        prompt = hot[at(chunk), :]
+        places = span + lax.rem(line, steps)
+        for p in range(n_rep):
+            places = places + jnp.where(prompt == p, length[p], 0)
+        angles(chunk + span_blocks, places)
+
+    loads[2].wait()
+    strip = lax.broadcasted_iota(jnp.int32, (page_size, HD), 0)
+    strip_lane = lax.broadcasted_iota(jnp.int32, (page_size, HD), 1)
+    for page in range(pages):
+        entry = jnp.int32(0)
+        for index in range(pages):
+            entry = jnp.where(table[index] == page, index, entry)
+        prompt = entry // cpages
+        seen = strip + lax.rem(entry, cpages) * page_size < length[prompt]
+        here = slice(page * page_size, (page + 1) * page_size)
+        keys[here, :HD] = pool[page, :, :HD]
+        values[here, :HD] = pool[page, :, HD:]
+        good = (seen & (strip_lane == prompt)) | (strip_lane >= n_rep)
+        keys[here, HD:] = jnp.where(good, 0.0, FAR).astype(jnp.bfloat16)
+    for p in range(n_rep):
+        block_lane = lax.broadcasted_iota(jnp.int32, (span, HD), 1)
+        good = (block_lane == owner_of[p]) | (block_lane >= n_rep)
+        keys[cached + p * span : cached + (p + 1) * span, HD:] = jnp.where(good, 0.0, FAR).astype(
+            jnp.bfloat16
+        )
     values[:, HD:] = jnp.ones((values.shape[0], HD), jnp.bfloat16)
     tail_value[:, HD:] = jnp.ones((TILE, HD), jnp.bfloat16)
 
+    for block in range(1, span_blocks + 1):
+        forward(block)
+
     def reduced(block):
-        total = own[at(block), :]
-        for k in range(1, n):
-            rs_copy(k, block).wait_recv()
-            total = total + landed[k - 1, at(block), :].astype(jnp.float32)
+        for side, inside in ((0, z > 0), (1, z < n - 1)):
+
+            @pl.when(inside)
+            def _():
+                rs_copy(side, z, block).wait_recv()
+                mine[z, at(block), :] += landed[side, z, at(block), :].astype(jnp.float32)
+
+        total = mine[z, at(block), :]
         key = total[:, :HD]
         key = key * cosine[at(block), :] + pltpu.roll(key, HD // 2, 1) * sine[at(block), :]
         return key.astype(jnp.bfloat16), total[:, HD:].astype(jnp.bfloat16)
@@ -267,6 +370,7 @@
 
     for k in range(1, n_rep):
         sp_copy(k, rep).start()
+    loads[1].wait()
     for k in range(1, n_rep):
         sp_copy(k, lax.rem(rep - k + n_rep, n_rep)).wait_recv()
     for p in range(n_rep):
@@ -284,9 +388,22 @@
             device_id_type=MESH_ID,
         )
 
-    line = lax.broadcasted_iota(jnp.int32, (TILE, TILE), 0)
-    lane = lax.broadcasted_iota(jnp.int32, (TILE, TILE), 1)
-    causal = (line // steps == lane // steps) & (lane <= line)
+    def relay(distance, chunk):
+        for side, origin, inside, further in (
+            (0, z - distance, z >= distance, z + 1 < n),
+            (1, z + distance, z + distance < n, z > 0),
+        ):
+
+            @pl.when(inside)
+            def _():
+                ag_copy(side, distance, chunk, origin).wait_recv()
+
+            if distance < n - 1:
+
+                @pl.when(inside & further)
+                def _():
+                    ag_copy(side, distance + 1, chunk, origin).start()
+
     factor = math.log2(math.e) / math.sqrt(HD)
 
     @pl.loop(0, chunks)
@@ -294,12 +411,15 @@
         key, value = reduced(chunk + span_blocks)
         tail_key[...] = key
         tail_value[:, :HD] = value
-
-        @pl.loop(0, heads)
+        asked_all[...] = query[pl.ds(chunk * sampled, sampled)].reshape(TILE, width)
+        choice = (hot[at(chunk), :] == lane).astype(jnp.bfloat16)
+        causal = (line // steps == lane // steps) & (lane <= line)
+
+        @pl.loop(0, heads, unroll=2 if heads % 2 == 0 else 1)
         def _(head):
             column = pl.ds(pl.multiple_of(head * HD, HD), HD)
-            asked = query[at(chunk), column]
-            scores = nt(jnp.concatenate([asked, hot[at(chunk), :]], 1), keys[...])
+            asked = asked_all[:, column]
+            scores = nt(jnp.concatenate([asked, choice], 1), keys[...])
             tail = jnp.where(causal, nt(asked, tail_key[...]), FAR)
             highest = jnp.maximum(
                 jnp.max(scores, 1, keepdims=True), jnp.max(tail, 1, keepdims=True)
@@ -319,16 +439,25 @@
         def _():
             ag_copy(1, 1, chunk, z).start()
 
-    w_copy.wait()
-    tall = min(2 * TILE, rows)
+        @pl.when(chunk + span_blocks + 1 < blocks)
+        def _():
+            forward(chunk + span_blocks + 1)
+
+        @pl.when(chunk > 0)
+        def _():
+            relay(1, chunk - 1)
+
+    relay(1, chunks - 1)
+    loads[3].wait()
+    tall = min(2 * TILE, number)
     per = tall // TILE
-    wide = min(512, out.shape[1])
+    wide = min(512, acc.shape[1])
 
     def add(origin, half, first):
         span_rows = pl.ds(pl.multiple_of(half * tall, tall), tall)
         deep = pl.ds(pl.multiple_of(origin * width, width), width)
 
-        @pl.loop(0, out.shape[1] // wide)
+        @pl.loop(0, acc.shape[1] // wide)
         def _(column):
             cols = pl.ds(pl.multiple_of(column * wide, wide), wide)
             term = jnp.dot(
@@ -339,30 +468,17 @@
             else:
                 acc[span_rows, cols] += term
 
-    @pl.loop(0, rows // tall)
+    @pl.loop(0, number // tall)
     def _(half):
         add(z, half, True)
 
     for distance in range(1, n):
 
-        @pl.loop(0, rows // tall)
+        @pl.loop(0, number // tall)
         def _(half):
-            for side, origin, inside, onward in (
-                (0, z - distance, z >= distance, z + 1 < n),
-                (1, z + distance, z + distance < n, z > 0),
-            ):
+            if distance > 1:
                 for piece in range(per):
-                    chunk = half * per + piece
-
-                    @pl.when(inside)
-                    def _():
-                        ag_copy(side, distance, chunk, origin).wait_recv()
-
-                    if distance < n - 1:
-
-                        @pl.when(inside & onward)
-                        def _():
-                            ag_copy(side, distance + 1, chunk, origin).start()
+                    relay(distance, half * per + piece)
 
             for side, origin, inside in (
                 (0, z - distance, z >= distance),
@@ -375,13 +491,18 @@
 
     @pl.loop(0, chunks)
     def _(chunk):
-        out[at(chunk), :] = acc[at(chunk), :].astype(jnp.bfloat16)
+        out[pl.ds(chunk * sampled, sampled)] = (
+            acc[at(chunk), :].astype(jnp.bfloat16).reshape(sampled, steps, acc.shape[1])
+        )
 
     for k in range(1, n):
-
-        @pl.loop(0, blocks)
-        def _(block):
-            rs_copy(k, block).wait_send()
+        for side, owner, inside in ((0, z + k, z + k < n), (1, z - k, z - k >= 0)):
+
+            @pl.when(inside)
+            def _():
+                @pl.loop(0, blocks)
+                def _(block):
+                    rs_copy(side, owner, block).wait_send()
 
     for k in range(1, n_rep):
         sp_copy(k, rep).wait_send()
@@ -411,7 +532,6 @@
     out_weight,
     page_pool,
 ):
-    replica = lax.axis_index("replica")
     n_replica = lax.axis_size("replica")
     n_tensor = lax.axis_size("tensor")
     span = span_states.shape[0]
@@ -425,92 +545,66 @@
         or number % TILE
         or number % min(2 * TILE, number)
         or TILE % steps
+        or 8 % steps
+        or rows % 8
         or n_replica > HD
     ):
         return general(
             prompt_owner, fork_map, page_table, prompt_length, span_states, decode_states,
             decode_queries, key_weight, value_weight, out_weight, page_pool,
         )
-    prompts = jnp.arange(n_replica, dtype=jnp.int32)
-    own_prompt = jnp.sum(jnp.where(prompts == replica, prompt_owner, 0))
-    own_length = jnp.sum(jnp.where(prompts == own_prompt, prompt_length, 0))
-    row_hits = fork_map[:, None] == prompts[None, :]
-    row_length = jnp.sum(jnp.where(row_hits, prompt_length[None, :], 0), 1)
-    positions = jnp.concatenate(
-        [
-            own_length + jnp.arange(span, dtype=jnp.int32),
-            (row_length[:, None] + span + jnp.arange(steps, dtype=jnp.int32)[None, :]).reshape(-1),
-        ]
-    )
     half = HD // 2
-    freq = rope_base ** (-(2.0 / HD) * jnp.arange(half, dtype=jnp.float32))
-    angle = positions.astype(jnp.float32)[:, None] * freq
-    cosine = jnp.cos(angle)
-    sine = jnp.sin(angle)
-    cosine = jnp.concatenate([cosine, cosine], 1)
-    sine = jnp.concatenate([-sine, sine], 1)
-    tokens = jnp.concatenate([span_states, decode_states.reshape(number, width)], 0)
-    pool_pages = page_table.shape[0]
-    cpages = pool_pages // n_replica
-    page_size = page_pool.shape[2]
-    entries = jnp.arange(pool_pages, dtype=jnp.int32)
-    page_hits = page_table[None, :] == entries[:, None]
-    page_prompt = jnp.sum(jnp.where(page_hits, entries[None, :] // cpages, 0), 1)
-    page_slot = jnp.sum(jnp.where(page_hits, entries[None, :] % cpages, 0), 1)
-    page_length = jnp.sum(
-        jnp.where(page_prompt[:, None] == prompts[None, :], prompt_length[None, :], 0), 1
-    )
-    visible = (
-        page_slot[:, None] * page_size + jnp.arange(page_size, dtype=jnp.int32)[None, :]
-        < page_length[:, None]
-    )
-    pool_prompt = jnp.where(visible, page_prompt[:, None], -1).reshape(-1)
-    key_prompt = jnp.concatenate([pool_prompt, jnp.repeat(prompt_owner, span)])
-    lanes = jnp.arange(HD, dtype=jnp.int32)
-    far = jnp.where(
-        (lanes[None, :] < n_replica) & (key_prompt[:, None] != lanes[None, :]), FAR, 0.0
-    ).astype(jnp.bfloat16)
-    hot = jnp.broadcast_to(
-        (fork_map[:, None] == lanes[None, :])[:, None, :], (rows, steps, HD)
-    ).reshape(number, HD).astype(jnp.bfloat16)
-    pool = page_pool.reshape(-1, 2 * HD)
-    query = decode_queries.reshape(number, heads_dev * HD)
+    freq = np.float64(rope_base) ** (-(2.0 / HD) * np.arange(half))
+    freq = jnp.asarray(np.tile(freq, (8, 2)), jnp.float32)
+    pages, page_size = page_pool.shape[1:3]
     features = out_weight.shape[1]
-    table = pool.shape[0] + n_replica * span
+    table = pages * page_size + n_replica * span
     total = span + number
     vmem = pl.BlockSpec(memory_space=pltpu.VMEM)
+    smem = pl.BlockSpec(memory_space=pltpu.SMEM)
+    hbm = pl.BlockSpec(memory_space=pl.ANY)
     bf16, f32 = jnp.bfloat16, jnp.float32
-    decoded = pl.pallas_call(
+    return pl.pallas_call(
         functools.partial(fused, n_tensor, n_replica, steps),
         name="fused",
-        out_shape=jax.ShapeDtypeStruct((number, features), bf16),
-        in_specs=[vmem] * 9 + [pl.BlockSpec(memory_space=pl.ANY)],
+        out_shape=jax.ShapeDtypeStruct((rows, steps, features), bf16),
+        in_specs=[smem] * 4 + [vmem] * 4 + [hbm] * 4,
         out_specs=vmem,
         scratch_shapes=[
             pltpu.VMEM(out_weight.shape, bf16),
-            pltpu.VMEM((n_tensor - 1, total, 2 * HD), bf16),
-            pltpu.VMEM((n_tensor - 1, total, 2 * HD), bf16),
-            pltpu.VMEM((total, 2 * HD), f32),
+            pltpu.VMEM(decode_states.shape, bf16),
+            pltpu.VMEM(decode_queries.shape, bf16),
+            pltpu.VMEM(page_pool.shape[1:], bf16),
+            pltpu.VMEM((total, width), bf16),
+            pltpu.VMEM((total, HD), f32),
+            pltpu.VMEM((total, HD), f32),
+            pltpu.VMEM((number, HD), jnp.int32),
+            pltpu.VMEM((n_tensor, total, 2 * HD), f32),
+            pltpu.VMEM((n_tensor, total, 2 * HD), bf16),
+            pltpu.VMEM((2, n_tensor, total, 2 * HD), bf16),
             pltpu.VMEM((n_replica, span, 2 * HD), bf16),
             pltpu.VMEM((table, 2 * HD), bf16),
             pltpu.VMEM((table, 2 * HD), bf16),
             pltpu.VMEM((TILE, HD), bf16),
             pltpu.VMEM((TILE, 2 * HD), bf16),
+            pltpu.VMEM((TILE, heads_dev * HD), bf16),
             pltpu.VMEM((n_tensor, number, heads_dev * HD), bf16),
             pltpu.VMEM((number, features), f32),
-            pltpu.SemaphoreType.DMA,
-            pltpu.SemaphoreType.DMA((n_tensor - 1, total // TILE)),
-            pltpu.SemaphoreType.DMA((n_tensor - 1, total // TILE)),
+            pltpu.SemaphoreType.DMA((4,)),
+            pltpu.SemaphoreType.DMA((n_tensor, total // TILE)),
+            pltpu.SemaphoreType.DMA((2, n_tensor, total // TILE)),
             pltpu.SemaphoreType.DMA((n_replica - 1,)),
             pltpu.SemaphoreType.DMA((n_replica - 1,)),
             pltpu.SemaphoreType.DMA((2, n_tensor - 1, number // TILE)),
             pltpu.SemaphoreType.DMA((2, n_tensor - 1, number // TILE)),
         ],
         compiler_params=pltpu.CompilerParams(
-            collective_id=0, has_side_effects=True, vmem_limit_bytes=60 * 1024 * 1024
+            collective_id=0, has_side_effects=True, vmem_limit_bytes=63 * 1024 * 1024
         ),
-    )(tokens, key_weight, value_weight, cosine, sine, query, hot, pool, far, out_weight)
-    return decoded.reshape(rows, steps, features)
+    )(
+        prompt_owner, fork_map, page_table, prompt_length, freq, span_states, key_weight,
+        value_weight, decode_states, decode_queries, page_pool[0], out_weight,
+    )
 
 
 def solution(mesh):

time: 142 us -> 147 us (1.035)
  Pallas kernels: 120 us -> 143 us
  other arithmetic: 12.5 us -> 0 us
  local copies, waits for them, and re-layouts: 9.24 us -> 3.92 us
    pallas_call x1, Pallas kernels: 120 us -> 143 us  [on_device(): pl.pallas_call(functools.partial(fused, n_tensor, n_replica, steps), name...]
    reshape x4 -> x0, local copies, waits for them, and re-layouts: 8.44 us -> none  [the longest x1 4.1 us: on_device(): return decoded.reshape(rows, steps, features)]
    reduce_sum x5 -> x0, other arithmetic: 5.67 us -> none  [the longest x1 2.02 us: on_device(): own_length = jnp.sum(jnp.where(prompts == own_prompt, prompt_length, 0))]
    unnamed x4 -> x1, local copies, waits for them, and re-layouts: 0.01 us -> 3.92 us
    concatenate x3 -> x0, other arithmetic: 2.79 us -> none  [the longest x1 1.68 us: on_device(): jnp.concatenate([span_states, decode_states.reshape(number, width)], 0)]
    convert_element_type x3 -> x0, other arithmetic: 1.91 us -> none  [the longest x1 1.16 us: on_device(): far = jnp.where((lanes[None, :] < n_replica) & (key_prompt[:, None] != la...]
where the time goes in v2:
time: 147 us
  Pallas kernels  143 us (97%)
  local copies, waits for them, and re-layouts  3.92 us (3%)
    pallas_call x1, Pallas kernels, on_device(): pl.pallas_call(functools.partial(fused, n_tensor, n_replica, steps), name...  143 us
    unnamed x1, local copies, waits for them, and re-layouts  3.92 us

profile of v2, /device:TPU:0, one launch (start us, length us, event | category | flops | bytes accessed | tf_op | source)
XLA Modules:
  0.0 146.9 jit_solution(1009833903812428213)
XLA Ops:
  0.0 142.9 %fused.1 = bf16[128,4,2048]{2,1,0:T(4,128)(2,1)} custom-call(s32[4]{0:T(128)} %owner_of.1, s32[128]{0:T(128)} %forks.1, s32[12]{0:T(128)} %table.1, s32[4]{0:T(128)} %length.1, f32[8,128]{1,0:T(8,128)} %constant.2.clone.freq, bf16[128,2048]{1,0:T(8,128)(2,1)} %first_tok.1, bf16[2048,512]{1,0:T(8,128)(2,1)} %wk.1, bf16[2048,512]{1,0:T(8,128)(2,1)} %wv.1, ...), custom_call_target="tpu_custom_call" | custom-call | tf_op jit(solution)/shard_map/fused/pallas_call | solution.py:567
  142.9 3.9 %copy.14 = bf16[128,4,2048]{2,1,0:T(4,128)(2,1)} copy(bf16[128,4,2048]{2,1,0:T(4,128)(2,1)} %fused.1) | data formatting | bytes 4194304
